TPU v7x, 32 devices: a whole 2x2x4 slice. The times are simulated.
32 devices in a mesh: dp: 32 (over z, y, x, core).
Axes of the slice: x: 2, y: 2, z: 4, core: 2. Of those that a mesh axis runs over, the one named last changes fastest.
Arguments:
- hidden: bfloat16 [24576, 2560], P('dp'), may hold values from -16 to 16
- rotation: bfloat16 [2560, 2560], P('dp'), may hold values from -1 to 1, as said below
- norm_gain: float32 [2, 2560], replicated, may hold values from 0.1 to 1.9
- value_weight: bfloat16 [2, 2560, 1024], P(None, None, 'dp'), may hold values from -0.125 to 0.125
- output_weight: bfloat16 [2, 1024, 2560], P(None, 'dp'), may hold values from -0.1875 to 0.1875
- lengths: int32 [32], replicated, may hold values from 1 to 768, as said below
Outputs:
- rotated_out: bfloat16 [24576, 2560], P('dp')
- calib_loss: float32 [], replicated
Inputs may be any that keep to these rules, and one draw needn't show every extreme that they name: `lengths`: some device has all of its 768 rows live. `rotation`: an orthogonal matrix rounded to bfloat16.
All inputs are finite; a program needn't handle non-finite values.
Results may differ from a plain program's by a relative error of at most 0.0088.
Values may be sent and summed in bfloat16 or wider, within the bound.
A program may use at most 192 MiB of HBM per device.

v0:
```python
import functools

import jax
import jax.numpy as jnp
from jax import lax
from jax.experimental import pallas as pl
from jax.experimental.pallas import tpu as pltpu
from jax.sharding import PartitionSpec as P

BLOCK = 256
CHUNK = 16
TILE = 512
VMEM_LIMIT = 60 * 1024 * 1024

EPS_NORM = 1e-06
EPS_SCALE = 1e-06
CLIP_RATIO = 0.9
POLY = (0.9999997571452157, -2.579687436847881, 2.6673586060553345, -1.5145036626283546, 0.48039577352173)


def soft_round(values):
    r = values - jnp.round(values)
    u = r * r
    p = jnp.float32(POLY[-1])
    for c in POLY[-2::-1]:
        p = p * u + jnp.float32(c)
    return values - p * (r - 4.0 * (r * u))


def fake_quant(values, step_size):
    inv = 1.0 / step_size
    return soft_round(jnp.clip(values * inv, -8.0, 7.0)) * step_size


def exchange_kernel(n, total, x_ref, out_ref, slots, send_sem, recv_sem):
    me = lax.axis_index("dp")
    barrier = pltpu.get_barrier_semaphore()

    def greet(k, _):
        pl.semaphore_signal(
            barrier,
            inc=1,
            device_id=(lax.rem(me + k, n),),
            device_id_type=pl.DeviceIdType.MESH,
        )
        return 0

    lax.fori_loop(1, n, greet, 0)
    pl.semaphore_wait(barrier, n - 1)

    def copy_to(peer, slot):
        return pltpu.make_async_remote_copy(
            src_ref=x_ref,
            dst_ref=slots.at[slot],
            send_sem=send_sem.at[peer],
            recv_sem=recv_sem.at[slot],
            device_id=(peer,),
            device_id_type=pl.DeviceIdType.MESH,
        )

    def push(k, _):
        copy_to(lax.rem(me + k, n), me).start()
        return 0

    lax.fori_loop(1, n, push, 0)
    slots[me] = x_ref[...]

    def settle(k, _):
        peer = lax.rem(me + k, n)
        copy = copy_to(peer, peer)
        copy.wait_send()
        copy.wait_recv()
        return 0

    lax.fori_loop(1, n, settle, 0)

    def fold(k, acc):
        return acc + slots[k] if total else jnp.maximum(acc, slots[k])

    out_ref[...] = lax.fori_loop(1, n, fold, slots[0])


def exchange(x, n, collective_id, total=False):
    return pl.pallas_call(
        functools.partial(exchange_kernel, n, total),
        name="exchange",
        in_specs=[pl.BlockSpec(memory_space=pltpu.VMEM)],
        out_specs=pl.BlockSpec(memory_space=pltpu.VMEM),
        out_shape=jax.ShapeDtypeStruct(x.shape, x.dtype),
        scratch_shapes=[
            pltpu.VMEM((n,) + x.shape, x.dtype),
            pltpu.SemaphoreType.DMA((n,)),
            pltpu.SemaphoreType.DMA((n,)),
        ],
        compiler_params=pltpu.CompilerParams(
            collective_id=collective_id, has_side_effects=True, vmem_limit_bytes=VMEM_LIMIT
        ),
        cost_estimate=pl.CostEstimate(flops=0, bytes_accessed=30_000_000, transcendentals=0),
    )(x)


def weight_kernel(v_rows, o_rows, layers, w_ref, r_ref, vq_ref, o_ref, top_ref, acc):
    j = pl.program_id(0)
    n = r_ref.shape[1]
    at = pl.ds(pl.multiple_of(j * n, n), n)
    prod = jnp.dot(w_ref[...], r_ref[...], preferred_element_type=jnp.float32)
    acc[:, at] = prod[:v_rows]
    o_ref[...] = prod[v_rows:]
    per = o_rows // layers
    for l in range(layers):
        lo = v_rows + l * per
        top_ref[l : l + 1, :] = jnp.max(jnp.abs(prod[lo : lo + per]), axis=0, keepdims=True)

    @pl.when(j == pl.num_programs(0) - 1)
    def _():
        def body(i, _):
            rows = pl.ds(pl.multiple_of(i * CHUNK, CHUNK), CHUNK)
            x = acc[rows, :]
            step = jnp.max(jnp.abs(x), axis=1, keepdims=True) / 7.0 + EPS_SCALE
            vq_ref[rows, :] = fake_quant(x, step).astype(jnp.bfloat16)
            return 0

        lax.fori_loop(0, v_rows // CHUNK, body, 0)


def rotate_weights(joined, rotation, v_rows, o_rows, layers):
    width = rotation.shape[1]
    depth = rotation.shape[0]
    return pl.pallas_call(
        functools.partial(weight_kernel, v_rows, o_rows, layers),
        name="rotate_weights",
        grid=(width // TILE,),
        in_specs=[
            pl.BlockSpec(joined.shape, lambda j: (0, 0)),
            pl.BlockSpec((depth, TILE), lambda j: (0, j)),
        ],
        out_specs=[
            pl.BlockSpec((v_rows, width), lambda j: (0, 0)),
            pl.BlockSpec((o_rows, TILE), lambda j: (0, j)),
            pl.BlockSpec((layers, TILE), lambda j: (0, j)),
        ],
        out_shape=[
            jax.ShapeDtypeStruct((v_rows, width), jnp.bfloat16),
            jax.ShapeDtypeStruct((o_rows, width), jnp.float32),
            jax.ShapeDtypeStruct((layers, width), jnp.float32),
        ],
        scratch_shapes=[pltpu.VMEM((v_rows, width), jnp.float32)],
        compiler_params=pltpu.CompilerParams(vmem_limit_bytes=VMEM_LIMIT),
        cost_estimate=pl.CostEstimate(
            flops=2 * joined.shape[0] * depth * width,
            bytes_accessed=2 * depth * width,
            transcendentals=0,
        ),
    )(joined, rotation)


def norm_rows(resid_ref, act_ref, msq_ref, aerr_ref):
    width = resid_ref.shape[1]

    def body(i, _):
        rows = pl.ds(pl.multiple_of(i * CHUNK, CHUNK), CHUNK)
        x = resid_ref[rows, :]
        mean_sq = jnp.sum(x * x, axis=1, keepdims=True) * (1.0 / width)
        inv = lax.rsqrt(mean_sq + EPS_NORM)
        step = CLIP_RATIO * (jnp.max(jnp.abs(x), axis=1, keepdims=True) * inv) / 7.0 + EPS_SCALE
        normed = x * inv
        act = fake_quant(normed, step)
        diff = act - normed
        act_ref[rows, :] = act.astype(jnp.bfloat16)
        msq_ref[rows, :] = mean_sq
        aerr_ref[rows, :] = jnp.sum(diff * diff, axis=1, keepdims=True)
        return 0

    lax.fori_loop(0, resid_ref.shape[0] // CHUNK, body, 0)


def first_kernel(h_ref, r_ref, resid_ref, act_ref, msq_ref, aerr_ref):
    def body(j, _):
        at = pl.ds(pl.multiple_of(j * TILE, TILE), TILE)
        resid_ref[:, at] = jnp.dot(h_ref[...], r_ref[:, at], preferred_element_type=jnp.float32)
        return 0

    lax.fori_loop(0, r_ref.shape[1] // TILE, body, 0)
    norm_rows(resid_ref, act_ref, msq_ref, aerr_ref)


def rows_spec(width):
    return pl.BlockSpec((BLOCK, width), lambda i, *_: (i, 0))


def whole_spec(shape):
    return pl.BlockSpec(shape, lambda i, *_: (0, 0), pipeline_mode=pl.Buffered(1))


def act_shapes(rows, width):
    return [
        jax.ShapeDtypeStruct((rows, width), jnp.float32),
        jax.ShapeDtypeStruct((rows, width), jnp.bfloat16),
        jax.ShapeDtypeStruct((rows, 1), jnp.float32),
        jax.ShapeDtypeStruct((rows, 1), jnp.float32),
    ]


def first_pass(hidden, rotation):
    rows, depth = hidden.shape
    width = rotation.shape[1]
    return pl.pallas_call(
        first_kernel,
        name="rotate_hidden",
        grid=(rows // BLOCK,),
        in_specs=[rows_spec(depth), whole_spec(rotation.shape)],
        out_specs=[rows_spec(width), rows_spec(width), rows_spec(1), rows_spec(1)],
        out_shape=act_shapes(rows, width),
        compiler_params=pltpu.CompilerParams(vmem_limit_bytes=VMEM_LIMIT),
        cost_estimate=pl.CostEstimate(
            flops=2 * rows * depth * width,
            bytes_accessed=2 * depth * width + 8 * rows * width,
            transcendentals=0,
        ),
    )(hidden, rotation)


def mix_kernel(len_ref, act_ref, v_ref, mixed_ref, top_ref):
    i = pl.program_id(0)
    tile = 256
    live = len_ref[0] - i * BLOCK
    mask = lax.broadcasted_iota(jnp.int32, (BLOCK, 1), 0) < live

    @pl.when(i == 0)
    def _():
        top_ref[...] = jnp.zeros_like(top_ref)

    cols = v_ref.shape[1]
    group = tile // cols

    def body(j, _):
        at = pl.ds(pl.multiple_of(j * tile, tile), tile)
        part = v_ref[pl.ds(j * group, group)]
        prod = lax.dot_general(
            act_ref[...],
            part.reshape(tile, part.shape[2]),
            (((1,), (1,)), ((), ())),
            preferred_element_type=jnp.float32,
        )
        mixed_ref[:, at] = prod
        peak = jnp.max(jnp.where(mask, jnp.abs(prod), 0.0), axis=0, keepdims=True)
        top_ref[:, at] = jnp.maximum(top_ref[:, at], peak)
        return 0

    lax.fori_loop(0, v_ref.shape[0] // group, body, 0)


def mix_pass(own_len, act, gathered, layer, cols):
    rows, width = act.shape
    n = gathered.shape[0]
    channels = n * cols
    if cols % 16 == 0:
        values = gathered
        spec = pl.BlockSpec(
            (n, cols, width), lambda i, *_: (0, layer, 0), pipeline_mode=pl.Buffered(1)
        )
    else:
        values = gathered[:, layer * cols : (layer + 1) * cols].reshape(-1, 128, width)
        spec = pl.BlockSpec(values.shape, lambda i, *_: (0, 0, 0), pipeline_mode=pl.Buffered(1))
    return pl.pallas_call(
        mix_kernel,
        name="mix",
        grid_spec=pltpu.PrefetchScalarGridSpec(
            num_scalar_prefetch=1,
            grid=(rows // BLOCK,),
            in_specs=[rows_spec(width), spec],
            out_specs=[
                rows_spec(channels),
                pl.BlockSpec((1, channels), lambda i, *_: (0, 0)),
            ],
        ),
        out_shape=[
            jax.ShapeDtypeStruct((rows, channels), jnp.float32),
            jax.ShapeDtypeStruct((1, channels), jnp.float32),
        ],
        compiler_params=pltpu.CompilerParams(vmem_limit_bytes=VMEM_LIMIT),
        cost_estimate=pl.CostEstimate(
            flops=2 * rows * channels * width,
            bytes_accessed=2 * channels * width + 4 * rows * width,
            transcendentals=0,
        ),
    )(own_len, act, values)


def update_kernel(last, len_ref, mixed_ref, vrange_ref, o_ref, resid_ref, msq_ref, aerr_ref, *rest):
    if last:
        loss_ref, out_ref, mix_buf = rest
    else:
        loss_ref, new_ref, act_ref, nmsq_ref, naerr_ref, mix_buf = rest
    live = len_ref[0] - pl.program_id(0) * BLOCK
    mask = lax.broadcasted_iota(jnp.int32, (BLOCK, 1), 0) < live
    step = CLIP_RATIO * vrange_ref[...] / 7.0 + EPS_SCALE

    def quant(i, _):
        rows = pl.ds(pl.multiple_of(i * CHUNK, CHUNK), CHUNK)
        x = mixed_ref[rows, :]
        mix = fake_quant(x, step)
        diff = mix - x
        mix_buf[rows, :] = mix.astype(jnp.bfloat16)
        loss_ref[rows, :] = jnp.sum(diff * diff, axis=1, keepdims=True)
        return 0

    lax.fori_loop(0, BLOCK // CHUNK, quant, 0)
    loss_ref[...] = jnp.where(mask, msq_ref[...] * (aerr_ref[...] + loss_ref[...]), 0.0)

    def body(j, _):
        at = pl.ds(pl.multiple_of(j * TILE, TILE), TILE)
        new = resid_ref[:, at] + jnp.dot(
            mix_buf[...], o_ref[:, at], preferred_element_type=jnp.float32
        )
        if last:
            out_ref[:, at] = jnp.where(mask, new, 0.0).astype(jnp.bfloat16)
        else:
            new_ref[:, at] = new
        return 0

    lax.fori_loop(0, o_ref.shape[1] // TILE, body, 0)
    if not last:
        norm_rows(new_ref, act_ref, nmsq_ref, naerr_ref)


def update_pass(own_len, mixed, vrange, outputs, resid, msq, aerr, last):
    rows, width = resid.shape
    channels = mixed.shape[1]
    out_specs = [rows_spec(1)]
    out_shape = [jax.ShapeDtypeStruct((rows, 1), jnp.float32)]
    if last:
        out_specs.append(rows_spec(width))
        out_shape.append(jax.ShapeDtypeStruct((rows, width), jnp.bfloat16))
    else:
        out_specs += [rows_spec(width), rows_spec(width), rows_spec(1), rows_spec(1)]
        out_shape += act_shapes(rows, width)
    return pl.pallas_call(
        functools.partial(update_kernel, last),
        name="update",
        grid_spec=pltpu.PrefetchScalarGridSpec(
            num_scalar_prefetch=1,
            grid=(rows // BLOCK,),
            in_specs=[
                rows_spec(channels),
                whole_spec((1, channels)),
                whole_spec(outputs.shape),
                rows_spec(width),
                rows_spec(1),
                rows_spec(1),
            ],
            out_specs=out_specs,
            scratch_shapes=[pltpu.VMEM((BLOCK, channels), jnp.bfloat16)],
        ),
        out_shape=out_shape,
        compiler_params=pltpu.CompilerParams(vmem_limit_bytes=VMEM_LIMIT),
        cost_estimate=pl.CostEstimate(
            flops=2 * rows * channels * width,
            bytes_accessed=2 * channels * width + 12 * rows * width,
            transcendentals=0,
        ),
    )(own_len, mixed, vrange, outputs, resid, msq, aerr)


def per_device(hidden, rotation, norm_gain, value_weight, output_weight, lengths):
    layers = norm_gain.shape[0]
    cols = value_weight.shape[2]
    own_len = lax.dynamic_slice_in_dim(lengths, lax.axis_index("dp"), 1)
    scaled = (norm_gain[:, :, None] * value_weight.astype(jnp.float32)).astype(jnp.bfloat16)
    width = rotation.shape[1]
    depth = value_weight.shape[1]
    joined = jnp.concatenate(
        [
            jnp.swapaxes(scaled, 1, 2).reshape(layers * cols, depth),
            output_weight.reshape(layers * cols, depth),
        ],
        axis=0,
    )
    rotation_full = lax.all_gather(rotation, "dp", axis=0, tiled=True)
    value_q, rotated_o, tops = rotate_weights(
        joined, rotation_full, layers * cols, layers * cols, layers
    )
    n = lax.axis_size("dp")
    tops = exchange(tops, n, 0)
    output_q = [
        fake_quant(
            rotated_o[l * cols : (l + 1) * cols], tops[l : l + 1] / 7.0 + EPS_SCALE
        ).astype(jnp.bfloat16)
        for l in range(layers)
    ]
    value_all = lax.all_gather(value_q, "dp", axis=0, tiled=False)
    output_all = []
    for l in range(layers):
        before = output_all[l - 1] if l > 0 else value_all
        local_o, _ = lax.optimization_barrier((output_q[l], before))
        output_all.append(lax.all_gather(local_o, "dp", axis=0, tiled=True))
    resid, act, msq, aerr = first_pass(hidden, rotation_full)
    loss = jnp.zeros((), jnp.float32)
    for l in range(layers):
        mixed, top = mix_pass(own_len, act, value_all, l, cols)
        vrange = exchange(top, n, 1)
        last = l == layers - 1
        res = update_pass(own_len, mixed, vrange, output_all[l], resid, msq, aerr, last)
        loss = loss + jnp.sum(res[0])
        if last:
            out = res[1]
        else:
            resid, act, msq, aerr = res[1:]
    count = jnp.sum(lengths).astype(jnp.float32)
    loss = exchange(jnp.full((1, 128), loss, jnp.float32), n, 2, total=True)[0, 0]
    return (out, loss / count)


def solution(mesh):
    return jax.shard_map(
        per_device,
        mesh=mesh,
        in_specs=(P("dp", None), P("dp", None), P(), P(None, None, "dp"), P(None, "dp", None), P()),
        out_specs=(P("dp", None), P()),
        check_vma=False,
    )
```

profile of v0, /device:TPU:0, one launch (start us, length us, event | category | flops | bytes accessed | tf_op | source)
XLA Modules:
  0.0 441.1 jit_solution(14004499083140990641)
XLA Ops:
  7.2 0.0 all-gather.6.cloned.1.call-start
  7.2 0.7 all-gather.6.cloned.1.call-update
  7.9 0.0 all-gather.12.cloned.1.call-start
  7.9 1.0 multiply_convert_fusion
  9.0 1.9 pad_maximum_fusion.w_ref
  10.8 0.0 copy-start.1
  10.8 100.4 %all-gather.6.cloned.1.call-done.r_ref = bf16[2560,2560]{1,0:T(8,128)(2,1)} async-done(((bf16[80,2560]{1,0:T(8,128)(2,1)}), bf16[2560,2560]{1,0:T(8,128)(2,1)}) %all-gather.6.cloned.1.call-update) | async-done | bytes 13107216 | tf_op jit(solution)/shard_map/all_gather | solution.py:379
  111.3 9.6 %rotate_weights.1 = (bf16[64,2560]{1,0:T(8,128)(2,1)}, f32[64,2560]{1,0:T(8,128)}, f32[2,2560]{1,0:T(2,128)}) custom-call(bf16[128,2560]{1,0:T(8,128)(2,1)} %pad_maximum_fusion.w_ref, bf16[2560,2560]{1,0:T(8,128)(2,1)} %all-gather.6.cloned.1.call-done.r_ref), custom_call_target="tpu_custom_call" | custom-call | flops 1677721600 | bytes 13107200 | tf_op jit(solution)/shard_map/rotate_weights/pallas_call | solution.py:129
  120.9 0.0 all-gather.12.cloned.1.call-update
  120.9 0.0 all-gather.8.cloned.1.call-start
  121.0 21.1 %exchange.5 = f32[2,2560]{1,0:T(2,128)} custom-call(f32[2,2560]{1,0:T(2,128)} %get-tuple-element.27.x_ref), custom_call_target="tpu_custom_call" | custom-call | bytes 30000000 | tf_op jit(solution)/shard_map/exchange/pallas_call | solution.py:84
  142.1 0.9 divide_reduce_fusion
  143.0 2.2 fusion.18
  145.3 66.7 %all-gather.12.cloned.1.call-done = bf16[2048,2560]{1,0:T(8,128)(2,1)} async-done(((bf16[64,2560]{1,0:T(8,128)(2,1)}), bf16[2048,2560]{1,0:T(8,128)(2,1)}) %all-gather.12.cloned.1.call-update) | async-done | bytes 10485776 | tf_op jit(solution)/shard_map/all_gather | solution.py:391
  211.9 0.0 all-gather.8.cloned.1.call-update
  211.9 0.0 all-gather.10.cloned.1.call-start
  212.0 67.2 %all-gather.8.cloned.1.call-done.o_ref = bf16[1024,2560]{1,0:T(8,128)(2,1)} async-done(((bf16[32,2560]{1,0:T(8,128)(2,1)}), bf16[1024,2560]{1,0:T(8,128)(2,1)}) %all-gather.8.cloned.1.call-update) | async-done | bytes 5242896 | tf_op jit(solution)/shard_map/all_gather | solution.py:396
  279.2 0.0 all-gather.10.cloned.1.call-update
  279.3 0.0 copy-done.1
  279.3 0.6 reduce_sum.29
  279.9 0.6 dynamic_slice.3.len_ref
  281.1 35.8 %rotate_hidden.1 = (f32[768,2560]{1,0:T(8,128)}, bf16[768,2560]{1,0:T(8,128)(2,1)}, f32[768,1]{1,0:T(8,128)}, f32[768,1]{1,0:T(8,128)}) custom-call(bf16[768,2560]{1,0:T(8,128)(2,1)} %h_ref.1, bf16[2560,2560]{1,0:T(8,128)(2,1)} %all-gather.6.cloned.1.call-done.r_ref), custom_call_target="tpu_custom_call" | custom-call | flops 10066329600 | bytes 28835840 | tf_op jit(solution)/shard_map/rotate_hidden/pallas_call | solution.py:207
  317.0 11.3 %mix.2 = (f32[768,1024]{1,0:T(8,128)}, f32[1,1024]{1,0:T(1,128)}) custom-call(s32[1]{0:T(128)} %dynamic_slice.3.len_ref, bf16[768,2560]{1,0:T(8,128)(2,1)} %get-tuple-element.22.act_ref, bf16[32,64,2560]{2,1,0:T(8,128)(2,1)} %bitcast.9), custom_call_target="tpu_custom_call" | custom-call | flops 4026531840 | bytes 13107200 | tf_op jit(solution)/shard_map/mix/pallas_call | solution.py:265
  328.3 9.5 %exchange.4.vrange_ref = f32[1,1024]{1,0:T(1,128)} custom-call(f32[1,1024]{1,0:T(1,128)} %get-tuple-element.25.x_ref), custom_call_target="tpu_custom_call" | custom-call | bytes 30000000 | tf_op jit(solution)/shard_map/exchange/pallas_call | solution.py:84
  337.8 36.9 %update.2 = (f32[768,1]{1,0:T(8,128)}, f32[768,2560]{1,0:T(8,128)}, bf16[768,2560]{1,0:T(8,128)(2,1)}, f32[768,1]{1,0:T(8,128)}, f32[768,1]{1,0:T(8,128)}) custom-call(s32[1]{0:T(128)} %dynamic_slice.3.len_ref, f32[768,1024]{1,0:T(8,128)} %get-tuple-element.24.mixed_ref, f32[1,1024]{1,0:T(1,128)} %exchange.4.vrange_ref, ...), custom_call_target="tpu_custom_call" | custom-call | flops 4026531840 | bytes 28835840 | tf_op jit(solution)/shard_map/update/pallas_call | solution.py:338
  374.7 0.0 copy-start
  374.8 11.4 %mix.3 = (f32[768,1024]{1,0:T(8,128)}, f32[1,1024]{1,0:T(1,128)}) custom-call(s32[1]{0:T(128)} %dynamic_slice.3.len_ref, bf16[768,2560]{1,0:T(8,128)(2,1)} %get-tuple-element.32.act_ref, bf16[32,64,2560]{2,1,0:T(8,128)(2,1)} %bitcast.10), custom_call_target="tpu_custom_call" | custom-call | flops 4026531840 | bytes 13107200 | tf_op jit(solution)/shard_map/mix/pallas_call | solution.py:265
  386.1 12.6 %exchange.6.vrange_ref = f32[1,1024]{1,0:T(1,128)} custom-call(f32[1,1024]{1,0:T(1,128)} %get-tuple-element.34.x_ref), custom_call_target="tpu_custom_call" | custom-call | bytes 30000000 | tf_op jit(solution)/shard_map/exchange/pallas_call | solution.py:84
  398.8 0.0 copy-done
  398.8 0.7 reduce_sum.27
  399.5 0.0 all-gather.10.cloned.1.call-done.o_ref
  399.5 19.8 %update.3 = (f32[768,1]{1,0:T(8,128)}, bf16[768,2560]{1,0:T(8,128)(2,1)}) custom-call(s32[1]{0:T(128)} %dynamic_slice.3.len_ref, f32[768,1024]{1,0:T(8,128)} %get-tuple-element.33.mixed_ref, f32[1,1024]{1,0:T(1,128)} %exchange.6.vrange_ref, bf16[1024,2560]{1,0:T(8,128)(2,1)} %all-gather.10.cloned.1.call-done.o_ref, f32[768,2560]{1,0:T(8,128)} %get-tuple-element.36.resid_ref, ...), custom_call_target="tpu_custom_call" | custom-call | flops 4026531840 | bytes 28835840 | tf_op jit(solution)/shard_map/update/pallas_call | solution.py:338
  419.3 1.7 reduce_sum.28
  422.3 0.5 broadcast_in_dim.4.x_ref
  422.8 10.0 %exchange.7 = f32[1,128]{1,0:T(1,128)} custom-call(f32[1,128]{1,0:T(1,128)} %broadcast_in_dim.4.x_ref), custom_call_target="tpu_custom_call" | custom-call | bytes 30000000 | tf_op jit(solution)/shard_map/exchange/pallas_call | solution.py:84
Async XLA Ops:
  7.2 104.1 %all-gather.6.cloned.1.call-start = ((), (), s32[]{:S(2)}) async-start(), calls=%async_computation | async-start | bytes 13516800 | tf_op jit(solution)/shard_map/all_gather | solution.py:379
  7.9 204.0 %all-gather.12.cloned.1.call-start = ((), (), s32[]{:S(2)}) async-start(), calls=%async_computation.3 | async-start | bytes 10813440 | tf_op jit(solution)/shard_map/all_gather | solution.py:391
  10.8 268.4 %copy-start.1 = (s32[32]{0:T(128)S(1)}, s32[32]{0:T(128)}, u32[]{:S(2)}) copy-start(s32[32]{0:T(128)} %param.11) | copy-start | bytes 388
  120.9 158.3 %all-gather.8.cloned.1.call-start = ((), (), s32[]{:S(2)}) async-start(), calls=%async_computation.1 | async-start | bytes 5406720 | tf_op jit(solution)/shard_map/all_gather | solution.py:396
  211.9 187.6 %all-gather.10.cloned.1.call-start = ((), (), s32[]{:S(2)}) async-start(), calls=%async_computation.2 | async-start | bytes 5406720 | tf_op jit(solution)/shard_map/all_gather | solution.py:396
  374.7 24.0 %copy-start = (f32[768,1]{1,0:T(8,128)S(1)}, f32[768,1]{1,0:T(8,128)}, u32[]{:S(2)}) copy-start(f32[768,1]{1,0:T(8,128)} %get-tuple-element.40) | copy-start | bytes 9220
Sparse Core Ops, SparseCore 0:
  10.8 100.4 all-gather.5
  121.0 90.8 all-gather.11
  215.4 63.8 all-gather.7
  281.9 65.0 all-gather.9
where the time goes:
time: 442 us; the launch traced here: 441 us
  waiting for transfers between devices  235 us (53%)
  Pallas kernels  178 us (40%)
  between operations  17.5 us (4%)
  other arithmetic  9.07 us (2%)
    all_gather x1, waiting for transfers between devices, per_device(): rotation_full = lax.all_gather(rotation, 'dp', axis=0, tiled=True)  100 us
    all_gather x2, waiting for transfers between devices, per_device(): output_all.append(lax.all_gather(local_o, 'dp', axis=0, tiled=True))  67.2 us
    all_gather x1, waiting for transfers between devices, per_device(): value_all = lax.all_gather(value_q, 'dp', axis=0, tiled=False)  66.7 us
    pallas_call x2, Pallas kernels, update_pass(): pl.pallas_call(functools.partial(update_kernel, last), name='update', gri...  56.7 us
    pallas_call x4, Pallas kernels, exchange(): pl.pallas_call(functools.partial(exchange_kernel, n, total), name='exchan...  53.2 us
    pallas_call x1, Pallas kernels, first_pass(): pl.pallas_call(first_kernel, name='rotate_hidden', grid=(rows // BLOCK,),...  35.8 us
    pallas_call x2, Pallas kernels, mix_pass(): pl.pallas_call(mix_kernel, name='mix', grid_spec=pltpu.PrefetchScalarGrid...  22.7 us
    pallas_call x1, Pallas kernels, rotate_weights(): pl.pallas_call(functools.partial(weight_kernel, v_rows, o_rows, layers),...  9.61 us
  transfers between devices with their start and end apart: 4, of which 3 were waited for; matrix products, arithmetic and copies ran while one was open for 2% of the time, Pallas kernels for 31%

commit v1 on v0

--- a/solution.py
+++ b/solution.py
@@ -362,6 +362,535 @@
     )(own_len, mixed, vrange, outputs, resid, msq, aerr)
 
 
+MESH_ID = pl.DeviceIdType.MESH
+FULL_VMEM = 67043328
+PIECES = 3
+
+
+class Place:
+    def __init__(self, n):
+        me = lax.axis_index("dp")
+        core = lax.rem(me, 2)
+        self.me, self.planes, self.core = me, n // 8, core
+        self.z = me // 8
+        self.stride2 = 2 + 2 * core
+        self.stride3 = 4 - 2 * core
+        self.bit2 = lax.rem(me // self.stride2, 2)
+        self.bit3 = lax.rem(me // self.stride3, 2)
+        self.to = [
+            me + 8,
+            me - 8,
+            me + self.stride2 * (1 - 2 * self.bit2),
+            me + self.stride3 * (1 - 2 * self.bit3),
+            me + 1 - 2 * core,
+        ]
+
+    def origin(self, plane, flip2, flip3):
+        bit2 = 1 - self.bit2 if flip2 else self.bit2
+        bit3 = 1 - self.bit3 if flip3 else self.bit3
+        return 8 * plane + self.core + self.stride2 * bit2 + self.stride3 * bit3
+
+    def at_distance(self, s):
+        if s == 0:
+            return [(self.z, None)]
+        return [(self.z - s, self.z >= s), (self.z + s, self.z + s < self.planes)]
+
+    def on_planes(self, s, piece):
+        if s == 0:
+            piece(self.z)
+            return
+
+        def body(k, _):
+            plane = self.z - s + 2 * s * k
+            pl.when(jnp.logical_and(plane >= 0, plane < self.planes))(lambda: piece(plane))
+            return 0
+
+        lax.fori_loop(0, 2, body, 0)
+
+    def greet(self):
+        barrier = pltpu.get_barrier_semaphore()
+        peers = [8 * self.z + lax.rem(self.me + k, 8) for k in range(1, 8)]
+        peers += [lax.rem(self.me + 8 * k, 8 * self.planes) for k in range(1, self.planes)]
+        for peer in peers:
+            pl.semaphore_signal(barrier, inc=1, device_id=(peer,), device_id_type=MESH_ID)
+        pl.semaphore_wait(barrier, len(peers))
+
+
+def run_if(cond, fn):
+    if cond is None:
+        fn()
+    else:
+        pl.when(cond)(fn)
+
+
+def start(copy):
+    copy.start()
+
+
+def sent(copy):
+    copy.wait_send()
+
+
+class Gather:
+    def __init__(self, place, buf, send_sem, recv_sem):
+        self.place, self.buf, self.send_sem, self.recv_sem = place, buf, send_sem, recv_sem
+
+    def copy(self, o, d):
+        return pltpu.make_async_remote_copy(
+            src_ref=self.buf.at[o],
+            dst_ref=self.buf.at[o],
+            send_sem=self.send_sem.at[d, o // 2],
+            recv_sem=self.recv_sem.at[o],
+            device_id=(self.place.to[d],),
+            device_id_type=MESH_ID,
+        )
+
+    def arrived(self, o):
+        self.copy(o, 4).wait_recv()
+
+    def up(self, o, act):
+        pl.when(self.place.z < self.place.planes - 1)(lambda: act(self.copy(o, 0)))
+
+    def down(self, o, act):
+        pl.when(self.place.z > 0)(lambda: act(self.copy(o, 1)))
+
+    def own(self, act=start):
+        o = self.place.me
+        self.up(o, act)
+        self.down(o, act)
+        for d in (2, 3, 4):
+            act(self.copy(o, d))
+
+    def line(self, s, act=start):
+        for k, (plane, cond) in enumerate(self.place.at_distance(s)):
+
+            def go(k=k, plane=plane):
+                o = self.place.origin(plane, 0, 0)
+                if act is start:
+                    self.arrived(o)
+                (self.up if k == 0 else self.down)(o, act)
+                for d in (2, 3, 4):
+                    act(self.copy(o, d))
+
+            run_if(cond, go)
+
+    def second(self, s, act=start):
+        for plane, cond in self.place.at_distance(s):
+
+            def go(plane=plane):
+                o = self.place.origin(plane, 1, 0)
+                if act is start:
+                    self.arrived(o)
+                for d in (3, 4):
+                    act(self.copy(o, d))
+
+            run_if(cond, go)
+
+    def third(self, s, act=start):
+        for plane, cond in self.place.at_distance(s):
+
+            def go(plane=plane):
+                for flip2 in (0, 1):
+                    o = self.place.origin(plane, flip2, 1)
+                    if act is start:
+                        self.arrived(o)
+                    act(self.copy(o, 4))
+
+            run_if(cond, go)
+
+    def other_core(self, s):
+        for plane, cond in self.place.at_distance(s):
+
+            def go(plane=plane):
+                for q in range(4):
+                    self.arrived(8 * plane + 2 * q + 1 - self.place.core)
+
+            run_if(cond, go)
+
+    def steps(self):
+        return self.place.planes + 2
+
+    def step(self, t):
+        planes = self.place.planes
+        if t == 0:
+            self.own()
+        elif t < planes:
+            self.line(t)
+        if 1 <= t < planes + 1:
+            self.second(t - 1)
+        if t >= 2:
+            self.third(t - 2)
+            self.other_core(t - 2)
+
+    def drain(self):
+        self.own(sent)
+        for s in range(self.place.planes):
+            if s:
+                self.line(s, sent)
+            self.second(s, sent)
+            self.third(s, sent)
+
+
+class Exchange:
+    def __init__(self, place, total, near, far, near_send, near_recv, far_send, far_recv):
+        self.place, self.total, self.near, self.far = place, total, near, far
+        self.sems = (near_send, near_recv, far_send, far_recv)
+        self.spot = lax.rem(place.me, 8)
+
+    def near_copy(self, k, slot):
+        spot = lax.rem(self.spot + k, 8)
+        return pltpu.make_async_remote_copy(
+            src_ref=self.near.at[slot],
+            dst_ref=self.near.at[slot],
+            send_sem=self.sems[0].at[k],
+            recv_sem=self.sems[1].at[slot],
+            device_id=(8 * self.place.z + spot,),
+            device_id_type=MESH_ID,
+        )
+
+    def far_copy(self, k, slot):
+        plane = lax.rem(self.place.z + k, self.place.planes)
+        return pltpu.make_async_remote_copy(
+            src_ref=self.far.at[slot],
+            dst_ref=self.far.at[slot],
+            send_sem=self.sems[2].at[k],
+            recv_sem=self.sems[3].at[slot],
+            device_id=(8 * plane + self.spot,),
+            device_id_type=MESH_ID,
+        )
+
+    def fold(self, slots, count):
+        acc = slots[0]
+        for k in range(1, count):
+            acc = acc + slots[k] if self.total else jnp.maximum(acc, slots[k])
+        return acc
+
+    def begin(self, value):
+        self.near[self.spot] = value
+        for k in range(1, 8):
+            self.near_copy(k, self.spot).start()
+
+    def middle(self):
+        for k in range(1, 8):
+            self.near_copy(k, lax.rem(self.spot + k, 8)).wait_recv()
+        self.far[self.place.z] = self.fold(self.near, 8)
+        for k in range(1, self.place.planes):
+            self.far_copy(k, self.place.z).start()
+
+    def end(self):
+        for k in range(1, self.place.planes):
+            self.far_copy(k, lax.rem(self.place.z + k, self.place.planes)).wait_recv()
+        return self.fold(self.far, self.place.planes)
+
+    def drain(self):
+        for k in range(1, 8):
+            self.near_copy(k, self.spot).wait_send()
+        for k in range(1, self.place.planes):
+            self.far_copy(k, self.place.z).wait_send()
+
+
+def window_kernel(n, layers, *refs):
+    len_ref, h_ref, w_ref, r_ref, out_ref, loss_ref = refs[:6]
+    (rbuf, vbuf, obuf, resid, wacc, act, mixed, mixq, top, msq, aerr, lossrow) = refs[6:18]
+    (ntops, ftops, ntop, ftop, nloss, floss) = refs[18:24]
+    (local_sem, out_sem, rsend, rrecv, wsend, wrecv, xns, xnr, xfs, xfr) = refs[24:]
+    place = Place(n)
+    planes = place.planes
+    rows, width = resid.shape
+    cols = vbuf.shape[2]
+    channels = n * cols
+    depth = 8 * r_ref.shape[0]
+    lanes = 8 * cols
+    live = len_ref[place.me]
+
+    mine = pltpu.make_async_copy(r_ref, rbuf.at[place.me], local_sem)
+    mine.start()
+    place.greet()
+    mine.wait()
+
+    rot = Gather(place, rbuf, rsend, rrecv)
+
+    def rotate(first):
+        def piece(plane):
+            ks = pl.ds(pl.multiple_of(plane * depth, 128), depth)
+
+            def body(j, _):
+                at = pl.ds(pl.multiple_of(j * TILE, TILE), TILE)
+                part = rbuf[pl.ds(8 * plane, 8), :, at].reshape(depth, TILE)
+                a = jnp.dot(h_ref[:, ks], part, preferred_element_type=jnp.float32)
+                w = jnp.dot(w_ref[:, ks], part, preferred_element_type=jnp.float32)
+                if first:
+                    resid[:, at] = a
+                    wacc[:, at] = w
+                else:
+                    resid[:, at] += a
+                    wacc[:, at] += w
+                return 0
+
+            lax.fori_loop(0, width // TILE, body, 0)
+
+        return piece
+
+    for t in range(rot.steps()):
+        rot.step(t)
+        if t >= 2:
+            place.on_planes(t - 2, rotate(t == 2))
+
+    vrows = layers * cols
+    for l in range(layers):
+        for i in range(cols // CHUNK):
+            x = wacc[l * cols + i * CHUNK : l * cols + (i + 1) * CHUNK, :]
+            step = jnp.max(jnp.abs(x), axis=1, keepdims=True) / 7.0 + EPS_SCALE
+            vbuf[l, place.me, i * CHUNK : (i + 1) * CHUNK, :] = fake_quant(x, step).astype(jnp.bfloat16)
+
+    gathers = []
+    for l in range(layers):
+        gathers.append(Gather(place, vbuf.at[l], wsend.at[2 * l], wrecv.at[2 * l]))
+        gathers.append(Gather(place, obuf.at[l], wsend.at[2 * l + 1], wrecv.at[2 * l + 1]))
+
+    def make(i, total, near, far):
+        return Exchange(place, total, near, far, xns.at[i], xnr.at[i], xfs.at[i], xfr.at[i])
+
+    tops = make(0, False, ntops, ftops)
+    vranges = [make(1 + l, False, ntop.at[l], ftop.at[l]) for l in range(layers)]
+    losses = make(1 + layers, True, nloss, floss)
+
+    def norm(p):
+        lo, hi = rows // CHUNK * p // PIECES, rows // CHUNK * (p + 1) // PIECES
+
+        def body(i, _):
+            at = pl.ds(pl.multiple_of(i * CHUNK, CHUNK), CHUNK)
+            x = resid[at, :]
+            mean_sq = jnp.sum(x * x, axis=1, keepdims=True) * (1.0 / width)
+            inv = lax.rsqrt(mean_sq + EPS_NORM)
+            step = CLIP_RATIO * (jnp.max(jnp.abs(x), axis=1, keepdims=True) * inv) / 7.0 + EPS_SCALE
+            normed = x * inv
+            q = fake_quant(normed, step)
+            diff = q - normed
+            act[at, :] = q.astype(jnp.bfloat16)
+            msq[at, :] = mean_sq
+            aerr[at, :] = jnp.sum(diff * diff, axis=1, keepdims=True)
+            return 0
+
+        lax.fori_loop(lo, hi, body, 0)
+
+    def mix(l):
+        def piece(plane):
+            at = pl.ds(pl.multiple_of(plane * lanes, 128), lanes)
+            part = vbuf[l, pl.ds(8 * plane, 8)].reshape(lanes, width)
+            peak = jnp.zeros((1, lanes), jnp.float32)
+            for b in range(rows // BLOCK):
+                rs = slice(b * BLOCK, (b + 1) * BLOCK)
+                prod = lax.dot_general(
+                    act[rs, :], part, (((1,), (1,)), ((), ())), preferred_element_type=jnp.float32
+                )
+                mixed[rs, at] = prod
+                mask = lax.broadcasted_iota(jnp.int32, (BLOCK, 1), 0) < live - b * BLOCK
+                peak = jnp.maximum(
+                    peak, jnp.max(jnp.where(mask, jnp.abs(prod), 0.0), axis=0, keepdims=True)
+                )
+            top[:, at] = peak
+
+        return piece
+
+    def quantize_mixed(l, vrange):
+        step = CLIP_RATIO * vrange / 7.0 + EPS_SCALE
+
+        def body(i, _):
+            at = pl.ds(pl.multiple_of(i * CHUNK, CHUNK), CHUNK)
+            x = mixed[at, :]
+            q = fake_quant(x, step)
+            diff = q - x
+            mixq[at, :] = q.astype(jnp.bfloat16)
+            mask = lax.broadcasted_iota(jnp.int32, (CHUNK, 1), 0) < live - i * CHUNK
+            err = jnp.sum(diff * diff, axis=1, keepdims=True)
+            row = jnp.where(mask, msq[at, :] * (aerr[at, :] + err), 0.0)
+            if l == 0:
+                lossrow[at, :] = row
+            else:
+                lossrow[at, :] += row
+            return 0
+
+        lax.fori_loop(0, rows // CHUNK, body, 0)
+
+    def update(l):
+        def piece(plane):
+            ks = pl.ds(pl.multiple_of(plane * lanes, 128), lanes)
+
+            def body(j, _):
+                at = pl.ds(pl.multiple_of(j * TILE, TILE), TILE)
+                part = obuf[l, pl.ds(8 * plane, 8), :, at].reshape(lanes, TILE)
+                resid[:, at] += jnp.dot(mixq[:, ks], part, preferred_element_type=jnp.float32)
+                return 0
+
+            lax.fori_loop(0, width // TILE, body, 0)
+
+        return piece
+
+    normed, quantized = [0] * layers, [False] * layers
+    waiting = [[] for _ in gathers]
+    for k in range(planes * len(gathers) + 2):
+        for g, gather in enumerate(gathers):
+            t = k - planes * g
+            if 0 <= t < gather.steps():
+                gather.step(t)
+                if t >= 2:
+                    waiting[g].append(t - 2)
+        if k == 0:
+            tops.begin(
+                jnp.concatenate(
+                    [
+                        jnp.max(
+                            jnp.abs(wacc[vrows + l * cols : vrows + (l + 1) * cols, :]),
+                            axis=0,
+                            keepdims=True,
+                        )
+                        for l in range(layers)
+                    ],
+                    axis=0,
+                )
+            )
+        if k == 1:
+            tops.middle()
+        if k == 2:
+            peaks = tops.end()
+            for l in range(layers):
+                lo = vrows + l * cols
+                obuf[l, place.me] = fake_quant(
+                    wacc[lo : lo + cols, :], peaks[l : l + 1] / 7.0 + EPS_SCALE
+                ).astype(jnp.bfloat16)
+        for l in range(layers):
+            t = k - 2 * planes * l
+            ready = l == 0 or (quantized[l - 1] and t >= 1)
+            if ready and normed[l] < PIECES and t >= 0:
+                norm(normed[l])
+                normed[l] += 1
+            if normed[l] == PIECES:
+                for s in waiting[2 * l]:
+                    place.on_planes(s, mix(l))
+                waiting[2 * l] = []
+            if t == planes + 1:
+                vranges[l].begin(top[...])
+            if t == planes + 2:
+                vranges[l].middle()
+            if t == planes + 3:
+                quantize_mixed(l, vranges[l].end())
+                quantized[l] = True
+                if l == layers - 1:
+                    losses.begin(
+                        jnp.broadcast_to(jnp.sum(lossrow[...], axis=0, keepdims=True), (1, 128))
+                    )
+            if t == planes + 4 and l == layers - 1:
+                losses.middle()
+            if quantized[l]:
+                for s in waiting[2 * l + 1]:
+                    place.on_planes(s, update(l))
+                waiting[2 * l + 1] = []
+
+    for b in range(rows // BLOCK):
+        rs = slice(b * BLOCK, (b + 1) * BLOCK)
+
+        def body(j, _):
+            at = pl.ds(pl.multiple_of(j * TILE, TILE), TILE)
+            mask = lax.broadcasted_iota(jnp.int32, (BLOCK, 1), 0) < live - b * BLOCK
+            act[rs, at] = jnp.where(mask, resid[rs, at], 0.0).astype(jnp.bfloat16)
+            return 0
+
+        lax.fori_loop(0, width // TILE, body, 0)
+        pltpu.make_async_copy(act.at[rs], out_ref.at[rs], out_sem.at[b]).start()
+
+    count = len_ref[0]
+    for k in range(1, n):
+        count = count + len_ref[k]
+    loss_ref[...] = losses.end() / count.astype(jnp.float32)
+
+    rot.drain()
+    for gather in gathers:
+        gather.drain()
+    for exchanged in [tops, *vranges, losses]:
+        exchanged.drain()
+    for b in range(rows // BLOCK):
+        rs = slice(b * BLOCK, (b + 1) * BLOCK)
+        pltpu.make_async_copy(act.at[rs], out_ref.at[rs], out_sem.at[b]).wait()
+
+
+def window(lengths, hidden, joined, rotation, layers):
+    n = lengths.shape[0]
+    rows, width = hidden.shape
+    cols = joined.shape[0] // (2 * layers)
+    channels = n * cols
+    planes = n // 8
+    f32, bf16 = jnp.float32, jnp.bfloat16
+    dma = pltpu.SemaphoreType.DMA
+    kinds = 2 + layers
+    vmem = pl.BlockSpec(memory_space=pltpu.VMEM)
+    return pl.pallas_call(
+        functools.partial(window_kernel, n, layers),
+        name="window",
+        in_specs=[
+            pl.BlockSpec(memory_space=pltpu.SMEM),
+            vmem,
+            vmem,
+            pl.BlockSpec(memory_space=pl.ANY),
+        ],
+        out_specs=[pl.BlockSpec(memory_space=pl.ANY), vmem],
+        out_shape=[
+            jax.ShapeDtypeStruct((rows, width), bf16),
+            jax.ShapeDtypeStruct((1, 128), f32),
+        ],
+        scratch_shapes=[
+            pltpu.VMEM((n,) + rotation.shape, bf16),
+            pltpu.VMEM((layers, n, cols, width), bf16),
+            pltpu.VMEM((layers, n, cols, width), bf16),
+            pltpu.VMEM((rows, width), f32),
+            pltpu.VMEM((2 * layers * cols, width), f32),
+            pltpu.VMEM((rows, width), bf16),
+            pltpu.VMEM((rows, channels), f32),
+            pltpu.VMEM((rows, channels), bf16),
+            pltpu.VMEM((1, channels), f32),
+            pltpu.VMEM((rows, 1), f32),
+            pltpu.VMEM((rows, 1), f32),
+            pltpu.VMEM((rows, 1), f32),
+            pltpu.VMEM((8, layers, width), f32),
+            pltpu.VMEM((planes, layers, width), f32),
+            pltpu.VMEM((layers, 8, 1, channels), f32),
+            pltpu.VMEM((layers, planes, 1, channels), f32),
+            pltpu.VMEM((8, 1, 128), f32),
+            pltpu.VMEM((planes, 1, 128), f32),
+            dma,
+            dma((rows // BLOCK,)),
+            dma((5, n // 2)),
+            dma((n,)),
+            dma((2 * layers, 5, n // 2)),
+            dma((2 * layers, n)),
+            dma((kinds, 8)),
+            dma((kinds, 8)),
+            dma((kinds, planes)),
+            dma((kinds, planes)),
+        ],
+        compiler_params=pltpu.CompilerParams(
+            collective_id=3, has_side_effects=True, vmem_limit_bytes=FULL_VMEM
+        ),
+        cost_estimate=pl.CostEstimate(
+            flops=2 * rows * width * (width + 2 * layers * channels),
+            bytes_accessed=4 * rows * width,
+            transcendentals=0,
+        ),
+    )(lengths, hidden, joined, rotation)
+
+
+def fits(n, hidden, rotation, cols):
+    return (
+        n % 8 == 0
+        and cols % CHUNK == 0
+        and rotation.shape[0] % CHUNK == 0
+        and (8 * rotation.shape[0]) % 128 == 0
+        and (8 * cols) % 128 == 0
+        and hidden.shape[0] % BLOCK == 0
+        and rotation.shape[1] % TILE == 0
+    )
+
+
 def per_device(hidden, rotation, norm_gain, value_weight, output_weight, lengths):
     layers = norm_gain.shape[0]
     cols = value_weight.shape[2]
@@ -376,11 +905,14 @@
         ],
         axis=0,
     )
+    n = lax.axis_size("dp")
+    if fits(n, hidden, rotation, cols):
+        out, loss = window(lengths, hidden, joined, rotation, layers)
+        return (out, loss[0, 0])
     rotation_full = lax.all_gather(rotation, "dp", axis=0, tiled=True)
     value_q, rotated_o, tops = rotate_weights(
         joined, rotation_full, layers * cols, layers * cols, layers
     )
-    n = lax.axis_size("dp")
     tops = exchange(tops, n, 0)
     output_q = [
         fake_quant(

time: 442 us -> 237 us (0.54)
  waiting for transfers between devices: 235 us -> 0 us
  Pallas kernels: 178 us -> 227 us
  between operations: 17.5 us -> 1.82 us
  other arithmetic: 9.07 us -> 2.88 us
    all_gather x4 -> x0, waiting for transfers between devices: 234 us -> none  [the longest x1 100 us: per_device(): rotation_full = lax.all_gather(rotation, 'dp', axis=0, tiled=True)]
    pallas_call x10 -> x1, Pallas kernels: 178 us -> 227 us  [window(): pl.pallas_call(functools.partial(window_kernel, n, layers), name='window'...]
  transfers between devices with their start and end apart: 4 -> 0, of which waited for: 3 -> 0; matrix products, arithmetic and copies ran while one was open for 2% -> 0% of each run, Pallas kernels for 31% -> 0%
where the time goes in v1:
time: 237 us; the launch traced here: 236 us
  Pallas kernels  227 us (96%)
  local copies, waits for them, and re-layouts  4.29 us (2%)
  other arithmetic  2.88 us (1%)
    pallas_call x1, Pallas kernels, window(): pl.pallas_call(functools.partial(window_kernel, n, layers), name='window'...  227 us

profile of v1, /device:TPU:0, one launch (start us, length us, event | category | flops | bytes accessed | tf_op | source)
XLA Modules:
  0.0 236.4 jit_solution(6889433107483734305)
XLA Ops:
  0.6 1.0 multiply_convert_fusion
  1.7 1.9 pad_maximum_fusion.refs_2_
  3.5 227.4 %window.1 = (bf16[768,2560]{1,0:T(8,128)(2,1)}, f32[1,128]{1,0:T(1,128)}) custom-call(s32[32]{0:T(128)} %refs_0_.1, bf16[768,2560]{1,0:T(8,128)(2,1)} %refs_1_.1, bf16[128,2560]{1,0:T(8,128)(2,1)} %pad_maximum_fusion.refs_2_, bf16[80,2560]{1,0:T(8,128)(2,1)} %refs_3_.1), custom_call_target="tpu_custom_call" | custom-call | flops 26172456960 | bytes 7864320 | tf_op jit(solution)/shard_map/window/pallas_call | solution.py:827
  230.9 0.0 copy-start
  230.9 4.3 %copy.10 = bf16[768,2560]{1,0:T(8,128)(2,1)} copy(bf16[768,2560]{1,0:T(8,128)(2,1)} %get-tuple-element.8) | data formatting | bytes 7864320
  235.2 0.0 copy-done
Async XLA Ops:
  230.9 4.3 %copy-start = (f32[1,128]{1,0:T(1,128)S(1)}, f32[1,128]{1,0:T(1,128)}, u32[]{:S(2)}) copy-start(f32[1,128]{1,0:T(1,128)} %get-tuple-element.5) | copy-start | bytes 1540

commit v2 on v1

--- a/solution.py
+++ b/solution.py
@@ -364,7 +364,13 @@
 
 MESH_ID = pl.DeviceIdType.MESH
 FULL_VMEM = 67043328
-PIECES = 3
+STRIP = 128
+ROT_TILE = 256
+LANES = 128
+HALVES = 2
+CROSS_TENTHS = 2
+ROT_STEP, ROT_GAP = 6.0, 12.0
+STEP, GAP = 6.0, 17.0
 
 
 class Place:
@@ -432,13 +438,14 @@
 
 
 class Gather:
-    def __init__(self, place, buf, send_sem, recv_sem):
+    def __init__(self, place, buf, send_sem, recv_sem, columns=slice(None)):
         self.place, self.buf, self.send_sem, self.recv_sem = place, buf, send_sem, recv_sem
+        self.columns = columns
 
     def copy(self, o, d):
         return pltpu.make_async_remote_copy(
-            src_ref=self.buf.at[o],
-            dst_ref=self.buf.at[o],
+            src_ref=self.buf.at[o, :, self.columns],
+            dst_ref=self.buf.at[o, :, self.columns],
             send_sem=self.send_sem.at[d, o // 2],
             recv_sem=self.recv_sem.at[o],
             device_id=(self.place.to[d],),
@@ -502,25 +509,26 @@
         for plane, cond in self.place.at_distance(s):
 
             def go(plane=plane):
-                for q in range(4):
+                def body(q, _):
                     self.arrived(8 * plane + 2 * q + 1 - self.place.core)
+                    return 0
+
+                lax.fori_loop(0, 4, body, 0)
 
             run_if(cond, go)
 
-    def steps(self):
-        return self.place.planes + 2
-
-    def step(self, t):
+    def events(self):
         planes = self.place.planes
-        if t == 0:
-            self.own()
-        elif t < planes:
-            self.line(t)
-        if 1 <= t < planes + 1:
-            self.second(t - 1)
-        if t >= 2:
-            self.third(t - 2)
-            self.other_core(t - 2)
+        out = [(0, self.own, None)]
+        for t in range(1, planes + 2):
+            if t < planes:
+                out.append((t, functools.partial(self.line, t), None))
+            if t < planes + 1:
+                out.append((t, functools.partial(self.second, t - 1), None))
+            if t >= 2:
+                out.append((t, functools.partial(self.third, t - 2), None))
+                out.append((t + 0.3, functools.partial(self.other_core, t - 2), t - 2))
+        return out
 
     def drain(self):
         self.own(sent)
@@ -529,6 +537,57 @@
                 self.line(s, sent)
             self.second(s, sent)
             self.third(s, sent)
+
+
+class Cross(Gather):
+    def second(self, act=start):
+        o = self.place.origin(self.place.z, 1, 0)
+        if act is start:
+            self.arrived(o)
+        self.up(o, act)
+        self.down(o, act)
+        for d in (3, 4):
+            act(self.copy(o, d))
+
+    def third(self, act=start):
+        for flip2 in (0, 1):
+            o = self.place.origin(self.place.z, flip2, 1)
+            if act is start:
+                self.arrived(o)
+            self.up(o, act)
+            self.down(o, act)
+            act(self.copy(o, 4))
+
+    def line(self, s, act=start):
+        for k, (plane, cond) in enumerate(self.place.at_distance(s)):
+
+            def go(k=k, plane=plane):
+                def body(q, _):
+                    o = 8 * plane + 2 * q + self.place.core
+                    if act is start:
+                        self.arrived(o)
+                    (self.up if k == 0 else self.down)(o, act)
+                    act(self.copy(o, 4))
+                    return 0
+
+                lax.fori_loop(0, 4, body, 0)
+
+            run_if(cond, go)
+
+    def events(self):
+        out = [(0, self.own, None), (0.5, self.second, None), (1.2, self.third, None)]
+        out.append((1.8, functools.partial(self.other_core, 0), 0))
+        for s in range(1, self.place.planes):
+            out.append((1.2 + s, functools.partial(self.line, s), None))
+            out.append((2.3 + s, functools.partial(self.other_core, s), s))
+        return out
+
+    def drain(self):
+        self.own(sent)
+        self.second(sent)
+        self.third(sent)
+        for s in range(1, self.place.planes):
+            self.line(s, sent)
 
 
 class Exchange:
@@ -589,11 +648,47 @@
             self.far_copy(k, self.place.z).wait_send()
 
 
+class Plan:
+    def __init__(self):
+        self.now, self.waits, self.work, self.count = 0.0, [], [], 0
+
+    def wait(self, when, action):
+        self.count += 1
+        self.waits.append((when, self.count, action))
+
+    def compute(self, rank, cost, action):
+        self.count += 1
+        self.work.append((rank, self.count, cost, action))
+
+    def run(self):
+        while self.waits or self.work:
+            self.waits.sort(key=lambda w: w[:2])
+            self.work.sort(key=lambda w: w[:2])
+            if self.waits and (not self.work or self.waits[0][0] <= self.now):
+                when, _, action = self.waits.pop(0)
+                self.now = max(self.now, when)
+                action()
+            else:
+                _, _, cost, action = self.work.pop(0)
+                action()
+                self.now += cost
+
+
+def soft_parts(scaled):
+    v = jnp.clip(scaled, -8.0, 7.0)
+    r = v - jnp.round(v)
+    u = r * r
+    p = jnp.float32(POLY[-1])
+    for c in POLY[-2::-1]:
+        p = p * u + jnp.float32(c)
+    return v - (p * (1.0 - 4.0 * u)) * r
+
+
 def window_kernel(n, layers, *refs):
     len_ref, h_ref, w_ref, r_ref, out_ref, loss_ref = refs[:6]
-    (rbuf, vbuf, obuf, resid, wacc, act, mixed, mixq, top, msq, aerr, lossrow) = refs[6:18]
-    (ntops, ftops, ntop, ftop, nloss, floss) = refs[18:24]
-    (local_sem, out_sem, rsend, rrecv, wsend, wrecv, xns, xnr, xfs, xfr) = refs[24:]
+    (rbuf, vbuf, obuf, resid, wacc, act, mixed, mixq, top, msq, aerr, lossrow, size, scale) = refs[6:20]
+    (ntops, ftops, ntop, ftop, nloss, floss) = refs[20:26]
+    (local_sem, out_sem, rsend, rrecv, wsend, wrecv, xns, xnr, xfs, xfr) = refs[26:]
     place = Place(n)
     planes = place.planes
     rows, width = resid.shape
@@ -601,52 +696,27 @@
     channels = n * cols
     depth = 8 * r_ref.shape[0]
     lanes = 8 * cols
+    half = width // HALVES
     live = len_ref[place.me]
+    strips = rows // STRIP
 
     mine = pltpu.make_async_copy(r_ref, rbuf.at[place.me], local_sem)
     mine.start()
     place.greet()
     mine.wait()
 
-    rot = Gather(place, rbuf, rsend, rrecv)
-
-    def rotate(first):
-        def piece(plane):
-            ks = pl.ds(pl.multiple_of(plane * depth, 128), depth)
-
-            def body(j, _):
-                at = pl.ds(pl.multiple_of(j * TILE, TILE), TILE)
-                part = rbuf[pl.ds(8 * plane, 8), :, at].reshape(depth, TILE)
-                a = jnp.dot(h_ref[:, ks], part, preferred_element_type=jnp.float32)
-                w = jnp.dot(w_ref[:, ks], part, preferred_element_type=jnp.float32)
-                if first:
-                    resid[:, at] = a
-                    wacc[:, at] = w
-                else:
-                    resid[:, at] += a
-                    wacc[:, at] += w
-                return 0
-
-            lax.fori_loop(0, width // TILE, body, 0)
-
-        return piece
-
-    for t in range(rot.steps()):
-        rot.step(t)
-        if t >= 2:
-            place.on_planes(t - 2, rotate(t == 2))
-
-    vrows = layers * cols
-    for l in range(layers):
-        for i in range(cols // CHUNK):
-            x = wacc[l * cols + i * CHUNK : l * cols + (i + 1) * CHUNK, :]
-            step = jnp.max(jnp.abs(x), axis=1, keepdims=True) / 7.0 + EPS_SCALE
-            vbuf[l, place.me, i * CHUNK : (i + 1) * CHUNK, :] = fake_quant(x, step).astype(jnp.bfloat16)
-
+    def both(buf, send_sem, recv_sem, lo, span):
+        cut = span * CROSS_TENTHS // 10 // 128 * 128
+        return (
+            Gather(place, buf, send_sem.at[0], recv_sem.at[0], pl.ds(lo, span - cut)),
+            Cross(place, buf, send_sem.at[1], recv_sem.at[1], pl.ds(lo + span - cut, cut)),
+        )
+
+    rots = [both(rbuf, rsend.at[q], rrecv.at[q], q * half, half) for q in range(HALVES)]
     gathers = []
     for l in range(layers):
-        gathers.append(Gather(place, vbuf.at[l], wsend.at[2 * l], wrecv.at[2 * l]))
-        gathers.append(Gather(place, obuf.at[l], wsend.at[2 * l + 1], wrecv.at[2 * l + 1]))
+        gathers.append(both(vbuf.at[l], wsend.at[2 * l], wrecv.at[2 * l], 0, width))
+        gathers.append(both(obuf.at[l], wsend.at[2 * l + 1], wrecv.at[2 * l + 1], 0, width))
 
     def make(i, total, near, far):
         return Exchange(place, total, near, far, xns.at[i], xnr.at[i], xfs.at[i], xfr.at[i])
@@ -654,22 +724,76 @@
     tops = make(0, False, ntops, ftops)
     vranges = [make(1 + l, False, ntop.at[l], ftop.at[l]) for l in range(layers)]
     losses = make(1 + layers, True, nloss, floss)
+    vrows = layers * cols
+
+    def product(q, left, total, first):
+        def piece(plane):
+            ks = pl.ds(pl.multiple_of(plane * depth, 128), depth)
+
+            def body(j, _):
+                at = pl.ds(pl.multiple_of(q * half + j * ROT_TILE, ROT_TILE), ROT_TILE)
+                part = rbuf[pl.ds(8 * plane, 8), :, at].reshape(depth, ROT_TILE)
+                prod = jnp.dot(left[:, ks], part, preferred_element_type=jnp.float32)
+                if first:
+                    total[:, at] = prod
+                else:
+                    total[:, at] += prod
+                return 0
+
+            lax.fori_loop(0, half // ROT_TILE, body, 0)
+
+        return piece
+
+    def quantize_values():
+        for l in range(layers):
+            for i in range(cols // CHUNK):
+                x = wacc[l * cols + i * CHUNK : l * cols + (i + 1) * CHUNK, :]
+                step = jnp.max(jnp.abs(x), axis=1, keepdims=True) / 7.0 + EPS_SCALE
+                vbuf[l, place.me, i * CHUNK : (i + 1) * CHUNK, :] = fake_quant(x, step).astype(jnp.bfloat16)
+
+    def begin_tops():
+        peaks = [
+            jnp.max(jnp.abs(wacc[vrows + l * cols : vrows + (l + 1) * cols, :]), axis=0, keepdims=True)
+            for l in range(layers)
+        ]
+        tops.begin(jnp.concatenate(peaks, axis=0))
+
+    def quantize_outputs():
+        peaks = tops.end()
+        for l in range(layers):
+            lo = vrows + l * cols
+            obuf[l, place.me] = fake_quant(
+                wacc[lo : lo + cols, :], peaks[l : l + 1] / 7.0 + EPS_SCALE
+            ).astype(jnp.bfloat16)
 
     def norm(p):
-        lo, hi = rows // CHUNK * p // PIECES, rows // CHUNK * (p + 1) // PIECES
-
-        def body(i, _):
-            at = pl.ds(pl.multiple_of(i * CHUNK, CHUNK), CHUNK)
-            x = resid[at, :]
-            mean_sq = jnp.sum(x * x, axis=1, keepdims=True) * (1.0 / width)
-            inv = lax.rsqrt(mean_sq + EPS_NORM)
-            step = CLIP_RATIO * (jnp.max(jnp.abs(x), axis=1, keepdims=True) * inv) / 7.0 + EPS_SCALE
-            normed = x * inv
-            q = fake_quant(normed, step)
-            diff = q - normed
-            act[at, :] = q.astype(jnp.bfloat16)
-            msq[at, :] = mean_sq
-            aerr[at, :] = jnp.sum(diff * diff, axis=1, keepdims=True)
+        at = pl.ds(pl.multiple_of(p * STRIP, STRIP), STRIP)
+        total = jnp.zeros((STRIP, LANES), jnp.float32)
+        peak = jnp.zeros((STRIP, LANES), jnp.float32)
+        for j in range(width // LANES):
+            x = resid[at, j * LANES : (j + 1) * LANES]
+            total = total + x * x
+            peak = jnp.maximum(peak, jnp.abs(x))
+        mean_sq = jnp.sum(total, axis=1, keepdims=True) * (1.0 / width)
+        inv = lax.rsqrt(mean_sq + EPS_NORM)
+        step = CLIP_RATIO * (jnp.max(peak, axis=1, keepdims=True) * inv) / 7.0 + EPS_SCALE
+        msq[at, :] = mean_sq
+        size[at, :] = step
+        scale[at, :] = inv / step
+        wide_step = jnp.broadcast_to(size[at, :], (STRIP, LANES))
+        wide_scale = jnp.broadcast_to(scale[at, :], (STRIP, LANES))
+        err = jnp.zeros((STRIP, LANES), jnp.float32)
+        for j in range(width // LANES):
+            scaled = resid[at, j * LANES : (j + 1) * LANES] * wide_scale
+            q = soft_parts(scaled)
+            act[at, j * LANES : (j + 1) * LANES] = (q * wide_step).astype(jnp.bfloat16)
+            diff = q - scaled
+            err = err + diff * diff
+        aerr[at, :] = jnp.sum(err, axis=1, keepdims=True) * (size[at, :] * size[at, :])
+
+    def norm_strips(lo, hi):
+        def body(p, _):
+            norm(p)
             return 0
 
         lax.fori_loop(lo, hi, body, 0)
@@ -693,25 +817,29 @@
 
         return piece
 
-    def quantize_mixed(l, vrange):
-        step = CLIP_RATIO * vrange / 7.0 + EPS_SCALE
-
-        def body(i, _):
-            at = pl.ds(pl.multiple_of(i * CHUNK, CHUNK), CHUNK)
-            x = mixed[at, :]
-            q = fake_quant(x, step)
-            diff = q - x
-            mixq[at, :] = q.astype(jnp.bfloat16)
-            mask = lax.broadcasted_iota(jnp.int32, (CHUNK, 1), 0) < live - i * CHUNK
-            err = jnp.sum(diff * diff, axis=1, keepdims=True)
-            row = jnp.where(mask, msq[at, :] * (aerr[at, :] + err), 0.0)
+    def quantize_mixed(l, lo, hi):
+        def body(p, _):
+            at = pl.ds(pl.multiple_of(p * STRIP, STRIP), STRIP)
+            err = jnp.zeros((STRIP, LANES), jnp.float32)
+            for j in range(channels // LANES):
+                cut = slice(j * LANES, (j + 1) * LANES)
+                step = CLIP_RATIO * top[:, cut] / 7.0 + EPS_SCALE
+                inv = 1.0 / step
+                x = mixed[at, cut]
+                q = soft_parts(x * inv) * step
+                mixq[at, cut] = q.astype(jnp.bfloat16)
+                diff = q - x
+                err = err + diff * diff
+            mask = lax.broadcasted_iota(jnp.int32, (STRIP, 1), 0) < live - p * STRIP
+            both = aerr[at, :] + jnp.sum(err, axis=1, keepdims=True)
+            row = jnp.where(mask, msq[at, :] * both, 0.0)
             if l == 0:
                 lossrow[at, :] = row
             else:
                 lossrow[at, :] += row
             return 0
 
-        lax.fori_loop(0, rows // CHUNK, body, 0)
+        lax.fori_loop(lo, hi, body, 0)
 
     def update(l):
         def piece(plane):
@@ -727,65 +855,117 @@
 
         return piece
 
-    normed, quantized = [0] * layers, [False] * layers
-    waiting = [[] for _ in gathers]
-    for k in range(planes * len(gathers) + 2):
-        for g, gather in enumerate(gathers):
-            t = k - planes * g
-            if 0 <= t < gather.steps():
-                gather.step(t)
-                if t >= 2:
-                    waiting[g].append(t - 2)
-        if k == 0:
-            tops.begin(
-                jnp.concatenate(
-                    [
-                        jnp.max(
-                            jnp.abs(wacc[vrows + l * cols : vrows + (l + 1) * cols, :]),
-                            axis=0,
-                            keepdims=True,
-                        )
-                        for l in range(layers)
-                    ],
-                    axis=0,
-                )
-            )
-        if k == 1:
-            tops.middle()
-        if k == 2:
-            peaks = tops.end()
-            for l in range(layers):
-                lo = vrows + l * cols
-                obuf[l, place.me] = fake_quant(
-                    wacc[lo : lo + cols, :], peaks[l : l + 1] / 7.0 + EPS_SCALE
-                ).astype(jnp.bfloat16)
-        for l in range(layers):
-            t = k - 2 * planes * l
-            ready = l == 0 or (quantized[l - 1] and t >= 1)
-            if ready and normed[l] < PIECES and t >= 0:
-                norm(normed[l])
-                normed[l] += 1
-            if normed[l] == PIECES:
-                for s in waiting[2 * l]:
-                    place.on_planes(s, mix(l))
-                waiting[2 * l] = []
-            if t == planes + 1:
-                vranges[l].begin(top[...])
-            if t == planes + 2:
-                vranges[l].middle()
-            if t == planes + 3:
-                quantize_mixed(l, vranges[l].end())
-                quantized[l] = True
-                if l == layers - 1:
-                    losses.begin(
-                        jnp.broadcast_to(jnp.sum(lossrow[...], axis=0, keepdims=True), (1, 128))
-                    )
-            if t == planes + 4 and l == layers - 1:
-                losses.middle()
-            if quantized[l]:
-                for s in waiting[2 * l + 1]:
-                    place.on_planes(s, update(l))
-                waiting[2 * l + 1] = []
+    plan = Plan()
+    held = [[] for _ in gathers]
+    open_ = [False] * len(gathers)
+
+    def gather_waits(pair, base, step, arrived):
+        here = [0] * planes
+        for gather in pair[::-1]:
+            for t, action, distance in gather.events():
+
+                def go(action=action, distance=distance):
+                    action()
+                    if distance is not None:
+                        here[distance] += 1
+                        if here[distance] == len(pair):
+                            arrived(distance)
+
+                plan.wait(base + step * t, go)
+
+    def rotated(q):
+        def arrived(s):
+            plan.compute(0, 0.3, lambda: (place.on_planes(s, product(q, w_ref, wacc, s == 0)), weights_done()))
+            plan.compute(1, 2.2, lambda: (place.on_planes(s, product(q, h_ref, resid, s == 0)), hidden_done()))
+
+        return arrived
+
+    counts = {"w": 0, "h": 0, "norm": [0] * layers, "mix": [0] * layers, "quant": [0] * layers, "upd": [0] * layers}
+
+    def weights_done():
+        counts["w"] += 1
+        if counts["w"] < HALVES * planes:
+            return
+        quantize_values()
+        base = plan.now
+        gather_waits(gathers[0], base, STEP, shards(0))
+        plan.wait(base + 0.1, begin_tops)
+        plan.wait(base + 4.0, tops.middle)
+
+        def outputs():
+            quantize_outputs()
+            for g in range(1, 2 * layers):
+                gather_waits(gathers[g], max(plan.now, base + GAP * g), STEP, shards(g))
+
+        plan.wait(base + 8.0, outputs)
+
+    def hidden_done():
+        counts["h"] += 1
+        if counts["h"] == HALVES * planes:
+            start_norm(0)
+
+    def start_norm(l):
+        for p in range(0, strips, 2):
+            plan.compute(2, 3.0, lambda p=p: (norm_strips(p, p + 2), norm_done(l)))
+
+    def norm_done(l):
+        counts["norm"][l] += 2
+        if counts["norm"][l] == strips:
+            release(2 * l)
+
+    def release(g):
+        open_[g] = True
+        for s in held[g]:
+            add_piece(g, s)
+        held[g] = []
+
+    def shards(g):
+        def arrived(s):
+            if open_[g]:
+                add_piece(g, s)
+            else:
+                held[g].append(s)
+
+        return arrived
+
+    def add_piece(g, s):
+        l = g // 2
+        if g % 2 == 0:
+            plan.compute(3, 1.3, lambda: (place.on_planes(s, mix(l)), mix_done(l)))
+        else:
+            plan.compute(5, 1.9, lambda: (place.on_planes(s, update(l)), update_done(l)))
+
+    def mix_done(l):
+        counts["mix"][l] += 1
+        if counts["mix"][l] < planes:
+            return
+        vranges[l].begin(top[...])
+        plan.wait(plan.now + 4.0, vranges[l].middle)
+
+        def end():
+            top[...] = vranges[l].end()
+            for p in range(0, strips, 2):
+                plan.compute(4, 1.2, lambda p=p: (quantize_mixed(l, p, p + 2), quant_done(l)))
+
+        plan.wait(plan.now + 8.0, end)
+
+    def quant_done(l):
+        counts["quant"][l] += 2
+        if counts["quant"][l] < strips:
+            return
+        if l == layers - 1:
+            losses.begin(jnp.broadcast_to(jnp.sum(lossrow[...], axis=0, keepdims=True), (1, 128)))
+            plan.wait(plan.now + 4.0, losses.middle)
+        release(2 * l + 1)
+
+    def update_done(l):
+        counts["upd"][l] += 1
+        if counts["upd"][l] == planes and l < layers - 1:
+            start_norm(l + 1)
+
+    for q in range(HALVES):
+        gather_waits(rots[q], q * ROT_GAP, ROT_STEP, rotated(q))
+    plan.run()
 
     for b in range(rows // BLOCK):
         rs = slice(b * BLOCK, (b + 1) * BLOCK)
@@ -804,9 +984,9 @@
         count = count + len_ref[k]
     loss_ref[...] = losses.end() / count.astype(jnp.float32)
 
-    rot.drain()
-    for gather in gathers:
-        gather.drain()
+    for pair in rots + gathers:
+        for gather in pair:
+            gather.drain()
     for exchanged in [tops, *vranges, losses]:
         exchanged.drain()
     for b in range(rows // BLOCK):
@@ -851,6 +1031,8 @@
             pltpu.VMEM((rows, 1), f32),
             pltpu.VMEM((rows, 1), f32),
             pltpu.VMEM((rows, 1), f32),
+            pltpu.VMEM((rows, 1), f32),
+            pltpu.VMEM((rows, 1), f32),
             pltpu.VMEM((8, layers, width), f32),
             pltpu.VMEM((planes, layers, width), f32),
             pltpu.VMEM((layers, 8, 1, channels), f32),
@@ -859,10 +1041,10 @@
             pltpu.VMEM((planes, 1, 128), f32),
             dma,
             dma((rows // BLOCK,)),
-            dma((5, n // 2)),
-            dma((n,)),
-            dma((2 * layers, 5, n // 2)),
-            dma((2 * layers, n)),
+            dma((HALVES, 2, 5, n // 2)),
+            dma((HALVES, 2, n)),
+            dma((2 * layers, 2, 5, n // 2)),
+            dma((2 * layers, 2, n)),
             dma((kinds, 8)),
             dma((kinds, 8)),
             dma((kinds, planes)),
@@ -888,6 +1070,8 @@
         and (8 * cols) % 128 == 0
         and hidden.shape[0] % BLOCK == 0
         and rotation.shape[1] % TILE == 0
+        and rotation.shape[1] % (HALVES * ROT_TILE) == 0
+        and hidden.shape[0] % (2 * STRIP) == 0
     )
 
 

time: 237 us -> 197 us (0.83)
  Pallas kernels: 227 us -> 188 us
    pallas_call x1, Pallas kernels: 227 us -> 188 us  [window(): pl.pallas_call(functools.partial(window_kernel, n, layers), name='window'...]
where the time goes in v2:
time: 197 us
  Pallas kernels  188 us (95%)
  local copies, waits for them, and re-layouts  4.29 us (2%)
  other arithmetic  2.88 us (1%)
    pallas_call x1, Pallas kernels, window(): pl.pallas_call(functools.partial(window_kernel, n, layers), name='window'...  188 us
    unnamed x3, local copies, waits for them, and re-layouts  4.29 us

profile of v2, /device:TPU:0, one launch (start us, length us, event | category | flops | bytes accessed | tf_op | source)
XLA Modules:
  0.0 196.8 jit_solution(12207084440326931214)
XLA Ops:
  0.6 1.0 multiply_convert_fusion
  1.7 1.9 pad_maximum_fusion.refs_2_
  3.5 187.8 %window.1 = (bf16[768,2560]{1,0:T(8,128)(2,1)}, f32[1,128]{1,0:T(1,128)}) custom-call(s32[32]{0:T(128)} %refs_0_.1, bf16[768,2560]{1,0:T(8,128)(2,1)} %refs_1_.1, bf16[128,2560]{1,0:T(8,128)(2,1)} %pad_maximum_fusion.refs_2_, bf16[80,2560]{1,0:T(8,128)(2,1)} %refs_3_.1), custom_call_target="tpu_custom_call" | custom-call | flops 26172456960 | bytes 7864320 | tf_op jit(solution)/shard_map/window/pallas_call | solution.py:1007
  191.3 0.0 copy-start
  191.3 4.3 %copy.10 = bf16[768,2560]{1,0:T(8,128)(2,1)} copy(bf16[768,2560]{1,0:T(8,128)(2,1)} %get-tuple-element.8) | data formatting | bytes 7864320
  195.6 0.0 copy-done
Async XLA Ops:
  191.3 4.3 %copy-start = (f32[1,128]{1,0:T(1,128)S(1)}, f32[1,128]{1,0:T(1,128)}, u32[]{:S(2)}) copy-start(f32[1,128]{1,0:T(1,128)} %get-tuple-element.5) | copy-start | bytes 1540

commit v3 on v2

--- a/solution.py
+++ b/solution.py
@@ -685,14 +685,17 @@
 
 
 def window_kernel(n, layers, *refs):
-    len_ref, h_ref, w_ref, r_ref, out_ref, loss_ref = refs[:6]
-    (rbuf, vbuf, obuf, resid, wacc, act, mixed, mixq, top, msq, aerr, lossrow, size, scale) = refs[6:20]
-    (ntops, ftops, ntop, ftop, nloss, floss) = refs[20:26]
-    (local_sem, out_sem, rsend, rrecv, wsend, wrecv, xns, xnr, xfs, xfr) = refs[26:]
+    len_ref, h_ref, gain_ref, v_ref, o_ref, r_ref, out_ref, loss_ref = refs[:8]
+    (rbuf, vbuf, obuf, left, acc, act, mixed, mixq, top, msq, aerr, lossrow, size, scale) = refs[8:22]
+    (ntops, ftops, ntop, ftop, nloss, floss) = refs[22:28]
+    (local_sem, out_sem, rsend, rrecv, wsend, wrecv, xns, xnr, xfs, xfr) = refs[28:]
     place = Place(n)
     planes = place.planes
-    rows, width = resid.shape
+    rows, width = act.shape
     cols = vbuf.shape[2]
+    vrows = layers * cols
+    resid = acc.at[pl.ds(0, rows), :]
+    wacc = acc.at[pl.ds(rows, 2 * vrows), :]
     channels = n * cols
     depth = 8 * r_ref.shape[0]
     lanes = 8 * cols
@@ -700,8 +703,14 @@
     live = len_ref[place.me]
     strips = rows // STRIP
 
-    mine = pltpu.make_async_copy(r_ref, rbuf.at[place.me], local_sem)
+    mine = pltpu.make_async_copy(r_ref, rbuf.at[place.me], local_sem.at[0])
     mine.start()
+    loads = [pltpu.make_async_copy(h_ref, left.at[pl.ds(0, rows), :], local_sem.at[1])]
+    for l in range(layers):
+        to = left.at[pl.ds(rows + vrows + l * cols, cols), :]
+        loads.append(pltpu.make_async_copy(o_ref.at[l], to, local_sem.at[2 + l]))
+    for load in loads:
+        load.start()
     place.greet()
     mine.wait()
 
@@ -724,9 +733,15 @@
     tops = make(0, False, ntops, ftops)
     vranges = [make(1 + l, False, ntop.at[l], ftop.at[l]) for l in range(layers)]
     losses = make(1 + layers, True, nloss, floss)
-    vrows = layers * cols
-
-    def product(q, left, total, first):
+
+    def prepare():
+        for l in range(layers):
+            scaled = gain_ref[l : l + 1, :] * v_ref[l].astype(jnp.float32)
+            left[rows + l * cols : rows + (l + 1) * cols, :] = scaled.astype(jnp.bfloat16)
+        for load in loads:
+            load.wait()
+
+    def product(q, first):
         def piece(plane):
             ks = pl.ds(pl.multiple_of(plane * depth, 128), depth)
 
@@ -735,9 +750,9 @@
                 part = rbuf[pl.ds(8 * plane, 8), :, at].reshape(depth, ROT_TILE)
                 prod = jnp.dot(left[:, ks], part, preferred_element_type=jnp.float32)
                 if first:
-                    total[:, at] = prod
+                    acc[:, at] = prod
                 else:
-                    total[:, at] += prod
+                    acc[:, at] += prod
                 return 0
 
             lax.fori_loop(0, half // ROT_TILE, body, 0)
@@ -841,19 +856,24 @@
 
         lax.fori_loop(lo, hi, body, 0)
 
+    def send_out(j):
+        at = pl.ds(pl.multiple_of(j * TILE, TILE), TILE)
+        return pltpu.make_async_copy(act.at[:, at], out_ref.at[:, at], out_sem.at[j])
+
     def update(l):
-        def piece(plane):
-            ks = pl.ds(pl.multiple_of(plane * lanes, 128), lanes)
-
-            def body(j, _):
-                at = pl.ds(pl.multiple_of(j * TILE, TILE), TILE)
-                part = obuf[l, pl.ds(8 * plane, 8), :, at].reshape(lanes, TILE)
-                resid[:, at] += jnp.dot(mixq[:, ks], part, preferred_element_type=jnp.float32)
-                return 0
-
-            lax.fori_loop(0, width // TILE, body, 0)
-
-        return piece
+        def body(j, _):
+            at = pl.ds(pl.multiple_of(j * TILE, TILE), TILE)
+            part = obuf[l, :, :, at].reshape(channels, TILE)
+            new = resid[:, at] + jnp.dot(mixq[...], part, preferred_element_type=jnp.float32)
+            if l == layers - 1:
+                mask = lax.broadcasted_iota(jnp.int32, (rows, 1), 0) < live
+                act[:, at] = jnp.where(mask, new, 0.0).astype(jnp.bfloat16)
+                send_out(j).start()
+            else:
+                resid[:, at] = new
+            return 0
+
+        lax.fori_loop(0, width // TILE, body, 0)
 
     plan = Plan()
     held = [[] for _ in gathers]
@@ -875,34 +895,29 @@
 
     def rotated(q):
         def arrived(s):
-            plan.compute(0, 0.3, lambda: (place.on_planes(s, product(q, w_ref, wacc, s == 0)), weights_done()))
-            plan.compute(1, 2.2, lambda: (place.on_planes(s, product(q, h_ref, resid, s == 0)), hidden_done()))
+            plan.compute(0, 2.5, lambda: (place.on_planes(s, product(q, s == 0)), rotation_done()))
 
         return arrived
 
-    counts = {"w": 0, "h": 0, "norm": [0] * layers, "mix": [0] * layers, "quant": [0] * layers, "upd": [0] * layers}
-
-    def weights_done():
-        counts["w"] += 1
-        if counts["w"] < HALVES * planes:
+    counts = {"rot": 0, "norm": [0] * layers, "mix": [0] * layers, "quant": [0] * layers, "out": [0] * layers}
+
+    def rotation_done():
+        counts["rot"] += 1
+        if counts["rot"] < HALVES * planes:
             return
         quantize_values()
         base = plan.now
         gather_waits(gathers[0], base, STEP, shards(0))
         plan.wait(base + 0.1, begin_tops)
-        plan.wait(base + 4.0, tops.middle)
+        plan.wait(base + 7.5, tops.middle)
 
         def outputs():
             quantize_outputs()
             for g in range(1, 2 * layers):
                 gather_waits(gathers[g], max(plan.now, base + GAP * g), STEP, shards(g))
 
-        plan.wait(base + 8.0, outputs)
-
-    def hidden_done():
-        counts["h"] += 1
-        if counts["h"] == HALVES * planes:
-            start_norm(0)
+        plan.wait(base + 12.0, outputs)
+        start_norm(0)
 
     def start_norm(l):
         for p in range(0, strips, 2):
@@ -932,22 +947,24 @@
         l = g // 2
         if g % 2 == 0:
             plan.compute(3, 1.3, lambda: (place.on_planes(s, mix(l)), mix_done(l)))
-        else:
-            plan.compute(5, 1.9, lambda: (place.on_planes(s, update(l)), update_done(l)))
+            return
+        counts["out"][l] += 1
+        if counts["out"][l] == planes:
+            plan.compute(5, 5.0, lambda: update_done(l))
 
     def mix_done(l):
         counts["mix"][l] += 1
         if counts["mix"][l] < planes:
             return
         vranges[l].begin(top[...])
-        plan.wait(plan.now + 4.0, vranges[l].middle)
+        plan.wait(plan.now + 2.5, vranges[l].middle)
 
         def end():
             top[...] = vranges[l].end()
             for p in range(0, strips, 2):
                 plan.compute(4, 1.2, lambda p=p: (quantize_mixed(l, p, p + 2), quant_done(l)))
 
-        plan.wait(plan.now + 8.0, end)
+        plan.wait(plan.now + 5.0, end)
 
     def quant_done(l):
         counts["quant"][l] += 2
@@ -959,25 +976,14 @@
         release(2 * l + 1)
 
     def update_done(l):
-        counts["upd"][l] += 1
-        if counts["upd"][l] == planes and l < layers - 1:
+        update(l)
+        if l < layers - 1:
             start_norm(l + 1)
 
+    plan.wait(0.2, prepare)
     for q in range(HALVES):
         gather_waits(rots[q], q * ROT_GAP, ROT_STEP, rotated(q))
     plan.run()
-
-    for b in range(rows // BLOCK):
-        rs = slice(b * BLOCK, (b + 1) * BLOCK)
-
-        def body(j, _):
-            at = pl.ds(pl.multiple_of(j * TILE, TILE), TILE)
-            mask = lax.broadcasted_iota(jnp.int32, (BLOCK, 1), 0) < live - b * BLOCK
-            act[rs, at] = jnp.where(mask, resid[rs, at], 0.0).astype(jnp.bfloat16)
-            return 0
-
-        lax.fori_loop(0, width // TILE, body, 0)
-        pltpu.make_async_copy(act.at[rs], out_ref.at[rs], out_sem.at[b]).start()
 
     count = len_ref[0]
     for k in range(1, n):
@@ -989,16 +995,16 @@
             gather.drain()
     for exchanged in [tops, *vranges, losses]:
         exchanged.drain()
-    for b in range(rows // BLOCK):
-        rs = slice(b * BLOCK, (b + 1) * BLOCK)
-        pltpu.make_async_copy(act.at[rs], out_ref.at[rs], out_sem.at[b]).wait()
-
-
-def window(lengths, hidden, joined, rotation, layers):
+    for j in range(width // TILE):
+        send_out(j).wait()
+
+
+def window(lengths, hidden, norm_gain, value_weight, output_weight, rotation):
     n = lengths.shape[0]
     rows, width = hidden.shape
-    cols = joined.shape[0] // (2 * layers)
+    layers, _, cols = value_weight.shape
     channels = n * cols
+    stacked = rows + 2 * layers * cols
     planes = n // 8
     f32, bf16 = jnp.float32, jnp.bfloat16
     dma = pltpu.SemaphoreType.DMA
@@ -1009,8 +1015,10 @@
         name="window",
         in_specs=[
             pl.BlockSpec(memory_space=pltpu.SMEM),
+            pl.BlockSpec(memory_space=pl.ANY),
             vmem,
             vmem,
+            pl.BlockSpec(memory_space=pl.ANY),
             pl.BlockSpec(memory_space=pl.ANY),
         ],
         out_specs=[pl.BlockSpec(memory_space=pl.ANY), vmem],
@@ -1022,8 +1030,8 @@
             pltpu.VMEM((n,) + rotation.shape, bf16),
             pltpu.VMEM((layers, n, cols, width), bf16),
             pltpu.VMEM((layers, n, cols, width), bf16),
-            pltpu.VMEM((rows, width), f32),
-            pltpu.VMEM((2 * layers * cols, width), f32),
+            pltpu.VMEM((stacked, width), bf16),
+            pltpu.VMEM((stacked, width), f32),
             pltpu.VMEM((rows, width), bf16),
             pltpu.VMEM((rows, channels), f32),
             pltpu.VMEM((rows, channels), bf16),
@@ -1039,8 +1047,8 @@
             pltpu.VMEM((layers, planes, 1, channels), f32),
             pltpu.VMEM((8, 1, 128), f32),
             pltpu.VMEM((planes, 1, 128), f32),
-            dma,
-            dma((rows // BLOCK,)),
+            dma((2 + layers,)),
+            dma((width // TILE,)),
             dma((HALVES, 2, 5, n // 2)),
             dma((HALVES, 2, n)),
             dma((2 * layers, 2, 5, n // 2)),
@@ -1058,7 +1066,7 @@
             bytes_accessed=4 * rows * width,
             transcendentals=0,
         ),
-    )(lengths, hidden, joined, rotation)
+    )(lengths, hidden, norm_gain, jnp.swapaxes(value_weight, 1, 2), output_weight, rotation)
 
 
 def fits(n, hidden, rotation, cols):
@@ -1078,6 +1086,10 @@
 def per_device(hidden, rotation, norm_gain, value_weight, output_weight, lengths):
     layers = norm_gain.shape[0]
     cols = value_weight.shape[2]
+    n = lax.axis_size("dp")
+    if fits(n, hidden, rotation, cols):
+        out, loss = window(lengths, hidden, norm_gain, value_weight, output_weight, rotation)
+        return (out, loss[0, 0])
     own_len = lax.dynamic_slice_in_dim(lengths, lax.axis_index("dp"), 1)
     scaled = (norm_gain[:, :, None] * value_weight.astype(jnp.float32)).astype(jnp.bfloat16)
     width = rotation.shape[1]
@@ -1089,10 +1101,6 @@
         ],
         axis=0,
     )
-    n = lax.axis_size("dp")
-    if fits(n, hidden, rotation, cols):
-        out, loss = window(lengths, hidden, joined, rotation, layers)
-        return (out, loss[0, 0])
     rotation_full = lax.all_gather(rotation, "dp", axis=0, tiled=True)
     value_q, rotated_o, tops = rotate_weights(
         joined, rotation_full, layers * cols, layers * cols, layers

time: 197 us -> 190 us (0.964)
  Pallas kernels: 188 us -> 183 us
  other arithmetic: 2.88 us -> 0 us
    pallas_call x1, Pallas kernels: 188 us -> 183 us  [window(): pl.pallas_call(functools.partial(window_kernel, n, layers), name='window'...]
where the time goes in v3:
time: 190 us; the launch traced here: 189 us
  Pallas kernels  183 us (96%)
  local copies, waits for them, and re-layouts  4.29 us (2%)
    pallas_call x1, Pallas kernels, window(): pl.pallas_call(functools.partial(window_kernel, n, layers), name='window'...  183 us
    unnamed x3, local copies, waits for them, and re-layouts  4.29 us

profile of v3, /device:TPU:0, one launch (start us, length us, event | category | flops | bytes accessed | tf_op | source)
XLA Modules:
  0.0 189.3 jit_solution(17121554830147345473)
XLA Ops:
  0.6 183.2 %window.1 = (bf16[768,2560]{1,0:T(8,128)(2,1)}, f32[1,128]{1,0:T(1,128)}) custom-call(s32[32]{0:T(128)} %refs_0_.1, bf16[768,2560]{1,0:T(8,128)(2,1)} %refs_1_.1, f32[2,2560]{1,0:T(2,128)} %refs_2_.1, bf16[2,32,2560]{2,1,0:T(8,128)(2,1)} %bitcast.3, bf16[2,32,2560]{2,1,0:T(8,128)(2,1)} %refs_4_.1, bf16[80,2560]{1,0:T(8,128)(2,1)} %refs_5_.1), custom_call_target="tpu_custom_call" | custom-call | flops 26172456960 | bytes 7864320 | tf_op jit(solution)/shard_map/window/pallas_call | solution.py:1013
  183.8 0.0 copy-start
  183.8 4.3 %copy.10 = bf16[768,2560]{1,0:T(8,128)(2,1)} copy(bf16[768,2560]{1,0:T(8,128)(2,1)} %get-tuple-element.8) | data formatting | bytes 7864320
  188.1 0.0 copy-done
Async XLA Ops:
  183.8 4.3 %copy-start = (f32[1,128]{1,0:T(1,128)S(1)}, f32[1,128]{1,0:T(1,128)}, u32[]{:S(2)}) copy-start(f32[1,128]{1,0:T(1,128)} %get-tuple-element.5) | copy-start | bytes 1540
